TPU v7x, 32 devices: a whole 2x2x4 slice. The times are simulated.
32 devices in a mesh: row: 4 (over z), col: 2 (over y), layer: 4 (over x, core).
Axes of the slice: x: 2, y: 2, z: 4, core: 2. Of those that a mesh axis runs over, the one named last changes fastest.
Arguments:
- tokens: bfloat16 [1280, 6144], P('row', 'layer'), may hold values from -6 to 6
- expert_ids: int32 [1280, 2], replicated, may hold values from 0 to 7, all different within a row; in each aligned block of 1280 rows (0 to 1279, 1280 to 2559, ...) at most 640 rows name the same one
- w_gate: bfloat16 [2, 6144, 8192], P(None, 'layer', ('row', 'col')), may hold values from -0.078125 to 0.078125
- w_up: bfloat16 [2, 6144, 8192], P(None, 'layer', ('row', 'col')), may hold values from -0.078125 to 0.078125
Outputs:
- hidden: bfloat16 [2, 640, 8192], P(None, ('col', 'layer'), 'row')
Inputs may be any that keep to these rules, and one draw needn't show every extreme that they name: `expert_ids`: each token names 2 different experts. No expert is named by more than 640 tokens, a bound that some block reaches.
All inputs are finite; a program needn't handle non-finite values.
Results may differ from a plain program's by a relative error of at most 0.0012.
Values may be sent and summed in bfloat16 or wider, within the bound.
A program may use at most 128 MiB of HBM per device.

v0:
```python
import jax
import jax.numpy as jnp
from jax import lax
from jax.sharding import PartitionSpec as P

SLOTS_DEV = 80


def passed_along(value, axis, steps):
    count = lax.axis_size(axis)
    pairs = [(source, (source + steps) % count) for source in range(count)]
    return lax.ppermute(value, axis, pairs)


def shards(tokens, expert_ids, w_gate, w_up):
    col_count = lax.axis_size("col")
    layer_count = lax.axis_size("layer")
    row_count = lax.axis_size("row")
    col_index = lax.axis_index("col")
    row_index = lax.axis_index("row")
    experts = w_gate.shape[0]
    capacity = SLOTS_DEV * col_count * layer_count
    slot_block = capacity // col_count
    local_rows = tokens.shape[0]
    tok_count = local_rows * row_count
    expert_range = jnp.arange(experts, dtype=jnp.int32)
    member = jnp.any(expert_ids[:, :, None] == expert_range[None, None, :], axis=1).astype(
        jnp.int32
    )
    slot_rank = jnp.cumsum(member, axis=0) - member
    target = jnp.where(member > 0, slot_rank, capacity)
    token_range = jnp.broadcast_to(jnp.arange(tok_count, dtype=jnp.int32)[:, None], target.shape)
    slot_table = (
        jnp.zeros((experts, capacity + 1), jnp.int32)
        .at[expert_range[None, :], target]
        .set(token_range)
    )
    counts = jnp.sum(member, axis=0)
    slot_start = col_index * slot_block
    picked = lax.dynamic_slice_in_dim(slot_table, slot_start, slot_block, 1)
    position = slot_start + jnp.arange(slot_block, dtype=jnp.int32)
    live_mask = position[None, :] < counts[:, None]
    row_start = row_index * local_rows
    local_pick = picked - row_start
    inside = live_mask & (local_pick >= 0) & (local_pick < local_rows)
    own_rows = tokens[jnp.clip(local_pick, 0, local_rows - 1)]
    placed = jnp.where(inside[:, :, None], own_rows, jnp.zeros((), tokens.dtype)).astype(
        jnp.float32
    )
    slot_rows = lax.psum(placed.astype(jnp.bfloat16), "row")
    stacked = jnp.stack((w_gate, w_up))
    narrow = w_gate.shape[2]
    totals = jnp.zeros((2, experts, slot_block, narrow * col_count), jnp.float32)
    moving = stacked
    for step in range(col_count):
        which_block = (col_index - step) % col_count
        totals = lax.dynamic_update_slice_in_dim(
            totals,
            jnp.einsum("ecd,pedf->pecf", slot_rows, moving, preferred_element_type=jnp.float32),
            which_block * narrow,
            3,
        )
        if step + 1 < col_count:
            moving = passed_along(moving, "col", 1)
    parts = lax.psum_scatter(totals, "layer", scatter_dimension=2, tiled=True)
    return (jax.nn.silu(parts[0]) * parts[1]).astype(jnp.bfloat16)


def solution(mesh):
    in_specs = (
        P("row", "layer"),
        P(),
        P(None, "layer", ("row", "col")),
        P(None, "layer", ("row", "col")),
    )
    out_specs = P(None, ("col", "layer"), "row")
    return jax.shard_map(shards, mesh=mesh, in_specs=in_specs, out_specs=out_specs, check_vma=False)
```

profile of v0, /device:TPU:0, one launch (start us, length us, event | category | flops | bytes accessed | tf_op | source)
XLA Modules:
  0.0 396.8 jit_solution(5306595772369583344)
XLA Ops:
  6.5 0.0 copy-start
  6.5 0.0 all-reduce.2.cloned.1.call-start
  6.5 0.0 copy-start.2
  6.5 0.0 copy-start.3
  6.5 0.0 copy-start.4
  6.6 10.5 %pad_maximum_fusion = bf16[2,2,1536,1024]{3,2,0,1:T(8,128)(2,1)} fusion(bf16[1,2,1536,1024]{3,2,0,1:T(8,128)(2,1)} %bitcast.45, bf16[1,2,1536,1024]{3,2,0,1:T(8,128)(2,1)} %bitcast.47), kind=kLoop, calls=%fused_computation.2 | loop fusion | flops 6291456 | bytes 25165824 | tf_op jit(solution)/shard_map/stack | solution.py:51
  17.0 3.0 collective-permute-start
  20.0 0.0 copy-done.2
  20.1 0.6 reduce-window.6
  20.7 0.2 slice_reduce_fusion
  20.9 0.2 reduce-window.9
  21.1 0.1 add_bitcast_fusion
  21.1 0.1 convert_reduce_fusion
  21.3 0.0 copy-done.3
  21.3 0.1 multiply_reduce_fusion
  21.4 0.0 copy-done.4
  21.4 0.1 and_reduce_fusion
  21.5 0.3 copy.15
  21.8 0.3 reshape.36
  22.1 0.3 reshape.38
  22.5 9.9 %scatter_custom_fusion = s32[1282]{0:T(1024)S(1)} fusion(s32[2560]{0:T(1024)S(1)} %reshape.36, s32[2560]{0:T(1024)S(1)} %reshape.38, s32[]{:T(128)} %constant.28.clone.1), kind=kCustom, calls=%fused_computation.31 | custom fusion | bytes 5132
  32.4 0.1 reshape.26
  32.5 0.1 compare_select_fusion.2
  32.5 0.1 reshape.30
  32.6 0.0 copy-done
  32.6 3.1 gather_fusion
  35.7 0.1 compare_and_fusion
  35.8 1.6 broadcast_select_fusion
  37.4 0.0 all-reduce.2.cloned.1.call-update
  37.4 0.0 reduce-scatter.2.cloned.1.call-start
  37.5 82.2 %all-reduce.2.cloned.1.call-done = bf16[2,320,1536]{2,1,0:T(8,128)(2,1)} async-done(((bf16[2,320,1536]{2,1,0:T(8,128)(2,1)}), bf16[2,320,1536]{2,1,0:T(8,128)(2,1)}) %all-reduce.2.cloned.1.call-update) | async-done | bytes 1966096 | tf_op jit(solution)/shard_map/psum | solution.py:50
  119.7 7.9 %convolution_bitcast_fusion.1 = f32[2,2,320,1024]{3,2,0,1:T(8,128)S(1)} fusion(bf16[2,320,1536]{2,1,0:T(8,128)(2,1)} %all-reduce.2.cloned.1.call-done, bf16[1,2,1536,1024]{3,2,0,1:T(8,128)(2,1)} %bitcast.46, bf16[1,2,1536,1024]{3,2,0,1:T(8,128)(2,1)} %bitcast.48), kind=kOutput, calls=%fused_computation.6 | convolution fusion | flops 4051697664 | bytes 19791872 | tf_op jit(solution)/shard_map/ecd,pedf->pecf/dot_general | solution.py:59
  127.6 5.2 %broadcast_in_dim.45 = f32[2,2,320,2048]{3,2,1,0:T(8,128)} broadcast(f32[]{:T(128)} %constant.20.clone.1), dimensions={} | broadcast | bytes 10485764 | tf_op jit(solution)/shard_map/broadcast_in_dim | solution.py:53
  132.8 0.0 copy-start.5
  132.8 2.7 copy_dynamic-update-slice_fusion.1
  135.5 155.2 %collective-permute-done = bf16[2,2,1536,1024]{3,2,0,1:T(8,128)(2,1)} collective-permute-done((bf16[2,2,1536,1024]{3,2,0,1:T(8,128)(2,1)}, bf16[2,2,1536,1024]{3,2,0,1:T(8,128)(2,1)}, u32[]{:S(2)}, u32[]{:S(2)}) %collective-permute-start) | collective-permute-done | bytes 12582944 | tf_op jit(solution)/shard_map/ppermute | solution.py:12
  290.7 0.0 copy-done.5
  290.7 7.4 %convolution_bitcast_fusion = f32[2,2,320,1024]{3,2,0,1:T(8,128)S(1)} fusion(bf16[2,2,1536,1024]{3,2,0,1:T(8,128)(2,1)} %collective-permute-done, bf16[2,320,1536]{2,1,0:T(8,128)(2,1)S(1)} %copy-done.5), kind=kOutput, calls=%fused_computation.5 | convolution fusion | flops 4026531840 | bytes 19791872 | tf_op jit(solution)/shard_map/ecd,pedf->pecf/dot_general | solution.py:59
  298.1 3.0 copy_dynamic-update-slice_fusion
  301.1 0.0 copy-start.1
  301.1 0.0 reduce-scatter.2.cloned.1.call-update
  301.1 86.0 %reduce-scatter.2.cloned.1.call-done = f32[2,2,80,2048]{3,2,1,0:T(8,128)} async-done(((f32[2,2,320,2048]{3,2,1,0:T(8,128)}), f32[2,2,80,2048]{3,2,1,0:T(8,128)}) %reduce-scatter.2.cloned.1.call-update) | async-done | bytes 2621456 | tf_op jit(solution)/shard_map/reduce_scatter | solution.py:65
  387.1 2.9 fusion.3
  390.0 0.0 copy-done.1
  (8 shorter events, 0.1 us)
Async XLA Ops:
  6.5 26.1 %copy-start = (bf16[320,1536]{1,0:T(8,128)(2,1)S(1)}, bf16[320,1536]{1,0:T(8,128)(2,1)}, u32[]{:S(2)}) copy-start(bf16[320,1536]{1,0:T(8,128)(2,1)} %param.4) | copy-start | bytes 2949124
  6.5 113.2 %all-reduce.2.cloned.1.call-start = ((), (), s32[]{:S(2)}) async-start(), calls=%async_computation.1 | async-start | bytes 3932160 | tf_op jit(solution)/shard_map/psum | solution.py:50
  6.5 13.5 %copy-start.2 = (s32[1280,2]{0,1:T(2,128)S(1)}, s32[1280,2]{0,1:T(2,128)}, u32[]{:S(2)}) copy-start(s32[1280,2]{0,1:T(2,128)} %param.5) | copy-start | bytes 30724
  6.5 14.7 %copy-start.3 = (s32[2]{0:T(128)S(1)}, s32[2]{0:T(128)}, u32[]{:S(2)}) copy-start(s32[2]{0:T(128)} %constant.63) | copy-start | bytes 28
  6.5 14.8 %copy-start.4 = (s32[2]{0:T(128)S(1)}, s32[2]{0:T(128)}, u32[]{:S(2)}) copy-start(s32[2]{0:T(128)} %constant.66) | copy-start | bytes 28
  17.0 273.6 %collective-permute-start = (bf16[2,2,1536,1024]{3,2,0,1:T(8,128)(2,1)}, bf16[2,2,1536,1024]{3,2,0,1:T(8,128)(2,1)}, u32[]{:S(2)}, u32[]{:S(2)}) collective-permute-start(bf16[2,2,1536,1024]{3,2,0,1:T(8,128)(2,1)} %pad_maximum_fusion), channel_id=1, source_target_pairs={{0,4},{4,0},{1,5},{5,1},{2,6},{6,2},{3,7},{7,3},{8,12},{12,8},{9,1... | collective-permute-start | bytes 37748744 | tf_op jit(solution)/shard_map/ppermute | solution.py:12
  37.4 349.6 %reduce-scatter.2.cloned.1.call-start = ((), (), s32[]{:S(2)}) async-start(), calls=%async_computation.2 | async-start | bytes 13107200 | tf_op jit(solution)/shard_map/reduce_scatter | solution.py:65
  132.8 157.9 %copy-start.5 = (bf16[2,320,1536]{2,1,0:T(8,128)(2,1)S(1)}, bf16[2,320,1536]{2,1,0:T(8,128)(2,1)}, u32[]{:S(2)}) copy-start(bf16[2,320,1536]{2,1,0:T(8,128)(2,1)} %all-reduce.2.cloned.1.call-done) | copy-start | bytes 5898244
  301.1 88.9 %copy-start.1 = (bf16[320,1536]{1,0:T(8,128)(2,1)S(1)}, bf16[320,1536]{1,0:T(8,128)(2,1)}, u32[]{:S(2)}) copy-start(bf16[320,1536]{1,0:T(8,128)(2,1)} %param.4) | copy-start | bytes 2949124
Sparse Core Ops, SparseCore 0:
  37.5 82.1 all-reduce.1
  301.2 85.7 reduce-scatter.1
where the time goes:
time: 397 us
  waiting for transfers between devices  323 us (81%)
  local copies, waits for them, and re-layouts  25.2 us (6%)
  other arithmetic  16.3 us (4%)
  matrix products  15.3 us (4%)
  between operations  13.6 us (3%)
    ppermute x1, waiting for transfers between devices, passed_along(): return lax.ppermute(value, axis, pairs)  155 us
    reduce_scatter x1, waiting for transfers between devices, shards(): parts = lax.psum_scatter(totals, 'layer', scatter_dimension=2, tiled=True)  86 us
    psum x1, waiting for transfers between devices, shards(): slot_rows = lax.psum(placed.astype(jnp.bfloat16), 'row')  82.2 us
    dot_general x2, matrix products, shards(): jnp.einsum('ecd,pedf->pecf', slot_rows, moving, preferred_element_type=jn...  15.3 us
    unnamed x15, local copies, waits for them, and re-layouts  10.5 us
    another operation x1, other arithmetic, shards(): stacked = jnp.stack((w_gate, w_up))  10.5 us
  transfers between devices with their start and end apart: 3, of which 3 were waited for; matrix products, arithmetic and copies ran while one was open for 8% of the time, Pallas kernels for 0%

commit v1 on v0

--- a/solution.py
+++ b/solution.py
@@ -13,6 +13,11 @@
 
 
 def shards(tokens, expert_ids, w_gate, w_up):
+
+    def chunk_fill(values, named_axis):
+        all_values = lax.all_gather(values, named_axis).sum(axis=0)
+        return all_values
+
     col_count = lax.axis_size("col")
     layer_count = lax.axis_size("layer")
     row_count = lax.axis_size("row")
@@ -47,7 +52,7 @@
     placed = jnp.where(inside[:, :, None], own_rows, jnp.zeros((), tokens.dtype)).astype(
         jnp.float32
     )
-    slot_rows = lax.psum(placed.astype(jnp.bfloat16), "row")
+    slot_rows = chunk_fill(placed.astype(jnp.bfloat16), "row")
     stacked = jnp.stack((w_gate, w_up))
     narrow = w_gate.shape[2]
     totals = jnp.zeros((2, experts, slot_block, narrow * col_count), jnp.float32)

time: 397 us -> 416 us (1.048)
  waiting for transfers between devices: 323 us -> 336 us
  other arithmetic: 16.3 us -> 23.4 us
    all_gather x0 -> x1, waiting for transfers between devices: none -> 130 us  [chunk_fill(): all_values = lax.all_gather(values, named_axis).sum(axis=0)]
    psum x1 -> x0, waiting for transfers between devices: 82.2 us -> none  [shards(): slot_rows = lax.psum(placed.astype(jnp.bfloat16), 'row')]
    ppermute x1, waiting for transfers between devices: 155 us -> 120 us  [passed_along(): return lax.ppermute(value, axis, pairs)]
    reduce_sum x0 -> x1, other arithmetic: none -> 5.1 us  [chunk_fill(): all_values = lax.all_gather(values, named_axis).sum(axis=0)]
    unnamed x15 -> x7, local copies, waits for them, and re-layouts: 10.5 us -> 10.5 us
  transfers between devices with their start and end apart: 3 -> 3, of which waited for: 3 -> 3; matrix products, arithmetic and copies ran while one was open for 8% -> 7% of each run, Pallas kernels for 0% -> 0%
where the time goes in v1:
time: 416 us
  waiting for transfers between devices  336 us (81%)
  local copies, waits for them, and re-layouts  25.2 us (6%)
  other arithmetic  23.4 us (6%)
  matrix products  14.5 us (3%)
  between operations  13.5 us (3%)
    all_gather x1, waiting for transfers between devices, chunk_fill(): all_values = lax.all_gather(values, named_axis).sum(axis=0)  130 us
    ppermute x1, waiting for transfers between devices, passed_along(): return lax.ppermute(value, axis, pairs)  120 us
    reduce_scatter x1, waiting for transfers between devices, shards(): parts = lax.psum_scatter(totals, 'layer', scatter_dimension=2, tiled=True)  86 us
    dot_general x2, matrix products, shards(): jnp.einsum('ecd,pedf->pecf', slot_rows, moving, preferred_element_type=jn...  14.5 us
    unnamed x7, local copies, waits for them, and re-layouts  10.5 us
    another operation x1, other arithmetic, shards(): stacked = jnp.stack((w_gate, w_up))  10.5 us
  transfers between devices with their start and end apart: 3, of which 3 were waited for; matrix products, arithmetic and copies ran while one was open for 7% of the time, Pallas kernels for 0%

profile of v1, /device:TPU:0, one launch (start us, length us, event | category | flops | bytes accessed | tf_op | source)
XLA Modules:
  0.0 416.1 jit_solution(274157988476845334)
XLA Ops:
  6.5 0.0 copy-start
  6.5 0.0 all-gather.2.cloned.1.call-start
  6.5 0.8 compare_reduce_fusion
  7.4 0.6 reduce-window.6
  8.0 0.2 slice_reduce_fusion
  8.2 0.2 reduce-window.9
  8.3 0.1 add_bitcast_fusion
  8.4 0.1 convert_reduce_fusion
  8.6 0.8 and_reduce_fusion
  9.3 0.7 multiply_reduce_fusion
  10.1 0.3 copy.15
  10.4 0.3 reshape.43
  10.7 0.3 reshape.45
  11.1 9.9 %scatter_custom_fusion = s32[1282]{0:T(1024)S(1)} fusion(s32[2560]{0:T(1024)S(1)} %reshape.43, s32[2560]{0:T(1024)S(1)} %reshape.45, s32[]{:T(128)} %constant.29.clone.1), kind=kCustom, calls=%fused_computation.31 | custom fusion | bytes 5132
  21.0 0.1 reshape.33
  21.1 0.1 compare_select_fusion.2
  21.1 0.1 reshape.37
  21.2 0.1 compare_and_fusion
  21.3 0.0 copy-done
  21.3 3.1 gather_fusion
  24.4 1.5 broadcast_select_fusion
  25.9 0.0 all-gather.2.cloned.1.call-update
  25.9 0.0 reduce-scatter.2.cloned.1.call-start
  26.0 10.5 %pad_maximum_fusion = bf16[2,2,1536,1024]{3,2,0,1:T(8,128)(2,1)} fusion(bf16[1,2,1536,1024]{3,2,0,1:T(8,128)(2,1)} %bitcast.46, bf16[1,2,1536,1024]{3,2,0,1:T(8,128)(2,1)} %bitcast.48), kind=kLoop, calls=%fused_computation.2 | loop fusion | flops 6291456 | bytes 25165824 | tf_op jit(solution)/shard_map/stack | solution.py:56
  36.4 3.2 collective-permute-start
  39.6 130.2 %all-gather.2.cloned.1.call-done = bf16[4,2,320,1536]{3,2,1,0:T(8,128)(2,1)} async-done(((bf16[1,2,320,1536]{3,2,1,0:T(8,128)(2,1)}), bf16[4,2,320,1536]{3,2,1,0:T(8,128)(2,1)}) %all-gather.2.cloned.1.call-update) | async-done | bytes 7864336 | tf_op jit(solution)/shard_map/all_gather | solution.py:18
  169.8 5.1 %reduce_sum.22 = bf16[2,320,1536]{2,1,0:T(8,128)(2,1)S(1)} reduce(bf16[4,2,320,1536]{3,2,1,0:T(8,128)(2,1)} %all-gather.2.cloned.1.call-done, bf16[]{:T(256)} %constant.58.clone.1), dimensions={0}, to_apply=%region_5.6 | reduce | flops 2949120 | bytes 9830402 | tf_op jit(solution)/shard_map/reduce_sum | solution.py:18
  175.0 7.3 %convolution_bitcast_fusion.1 = f32[2,2,320,1024]{3,2,0,1:T(8,128)S(1)} fusion(bf16[2,320,1536]{2,1,0:T(8,128)(2,1)S(1)} %reduce_sum.22, bf16[1,2,1536,1024]{3,2,0,1:T(8,128)(2,1)} %bitcast.47, bf16[1,2,1536,1024]{3,2,0,1:T(8,128)(2,1)} %bitcast.49), kind=kOutput, calls=%fused_computation.6 | convolution fusion | flops 4051697664 | bytes 19791872 | tf_op jit(solution)/shard_map/ecd,pedf->pecf/dot_general | solution.py:64
  182.2 5.2 %broadcast_in_dim.45 = f32[2,2,320,2048]{3,2,1,0:T(8,128)} broadcast(f32[]{:T(128)} %constant.21.clone.1), dimensions={} | broadcast | bytes 10485764 | tf_op jit(solution)/shard_map/broadcast_in_dim | solution.py:58
  187.5 2.7 copy_dynamic-update-slice_fusion.1
  190.1 120.1 %collective-permute-done = bf16[2,2,1536,1024]{3,2,0,1:T(8,128)(2,1)} collective-permute-done((bf16[2,2,1536,1024]{3,2,0,1:T(8,128)(2,1)}, bf16[2,2,1536,1024]{3,2,0,1:T(8,128)(2,1)}, u32[]{:S(2)}, u32[]{:S(2)}) %collective-permute-start) | collective-permute-done | bytes 12582944 | tf_op jit(solution)/shard_map/ppermute | solution.py:12
  310.2 7.2 %convolution_bitcast_fusion = f32[2,2,320,1024]{3,2,0,1:T(8,128)S(1)} fusion(bf16[2,2,1536,1024]{3,2,0,1:T(8,128)(2,1)} %collective-permute-done, bf16[2,320,1536]{2,1,0:T(8,128)(2,1)S(1)} %reduce_sum.22), kind=kOutput, calls=%fused_computation.5 | convolution fusion | flops 4026531840 | bytes 19791872 | tf_op jit(solution)/shard_map/ecd,pedf->pecf/dot_general | solution.py:64
  317.4 3.0 copy_dynamic-update-slice_fusion
  320.4 0.0 copy-start.1
  320.4 0.0 reduce-scatter.2.cloned.1.call-update
  320.4 86.0 %reduce-scatter.2.cloned.1.call-done = f32[2,2,80,2048]{3,2,1,0:T(8,128)} async-done(((f32[2,2,320,2048]{3,2,1,0:T(8,128)}), f32[2,2,80,2048]{3,2,1,0:T(8,128)}) %reduce-scatter.2.cloned.1.call-update) | async-done | bytes 2621456 | tf_op jit(solution)/shard_map/reduce_scatter | solution.py:70
  406.4 2.9 fusion.3
  409.3 0.0 copy-done.1
  (7 shorter events, 0.1 us)
Async XLA Ops:
  6.5 14.8 %copy-start = (bf16[320,1536]{1,0:T(8,128)(2,1)S(1)}, bf16[320,1536]{1,0:T(8,128)(2,1)}, u32[]{:S(2)}) copy-start(bf16[320,1536]{1,0:T(8,128)(2,1)} %param.4) | copy-start | bytes 2949124
  6.5 163.3 %all-gather.2.cloned.1.call-start = ((), (), s32[]{:S(2)}) async-start(), calls=%async_computation.1 | async-start | bytes 9830400 | tf_op jit(solution)/shard_map/all_gather | solution.py:18
  25.9 380.5 %reduce-scatter.2.cloned.1.call-start = ((), (), s32[]{:S(2)}) async-start(), calls=%async_computation.2 | async-start | bytes 13107200 | tf_op jit(solution)/shard_map/reduce_scatter | solution.py:70
  36.4 273.8 %collective-permute-start = (bf16[2,2,1536,1024]{3,2,0,1:T(8,128)(2,1)}, bf16[2,2,1536,1024]{3,2,0,1:T(8,128)(2,1)}, u32[]{:S(2)}, u32[]{:S(2)}) collective-permute-start(bf16[2,2,1536,1024]{3,2,0,1:T(8,128)(2,1)} %pad_maximum_fusion), channel_id=1, source_target_pairs={{0,4},{4,0},{1,5},{5,1},{2,6},{6,2},{3,7},{7,3},{8,12},{12,8},{9,1... | collective-permute-start | bytes 37748744 | tf_op jit(solution)/shard_map/ppermute | solution.py:12
  320.4 89.0 %copy-start.1 = (bf16[320,1536]{1,0:T(8,128)(2,1)S(1)}, bf16[320,1536]{1,0:T(8,128)(2,1)}, u32[]{:S(2)}) copy-start(bf16[320,1536]{1,0:T(8,128)(2,1)} %param.4) | copy-start | bytes 2949124
Sparse Core Ops, SparseCore 0:
  26.0 143.7 all-gather.1
  320.5 85.8 reduce-scatter.1
